TPU v7x, 256 devices: a whole 4x4x8 slice. The times are simulated.
256 devices in a mesh: freq: 8 (over z), tile: 32 (over x, y, core).
Axes of the slice: x: 4, y: 4, z: 8, core: 2. Of those that a mesh axis runs over, the one named last changes fastest.
Arguments:
- signal: bfloat16 [8, 2, 128, 16384], P('freq', None, None, 'tile'), may hold values from -6 to 6
- v_factors: bfloat16 [8, 64, 2, 48, 16384], P('freq', None, None, None, 'tile'), may hold values from -0.375 to 0.375
- u_factors: bfloat16 [8, 64, 2, 48, 16384], P('freq', None, None, None, 'tile'), may hold values from -0.0546875 to 0.0546875
- tile_ranks: int32 [8, 64, 64], P('freq'), may hold values from 16 to 48
- row_order: int32 [64], replicated, may hold values from 0 to 63, each once
- col_order: int32 [64], replicated, may hold values from 0 to 63, each once
- time_gate: float32 [2, 8, 8], replicated, may hold values from -1.5 to 1.5
Outputs:
- forward_data: bfloat16 [8, 2, 128, 16384], P('freq', None, None, 'tile')
- adjoint_data: bfloat16 [8, 2, 128, 16384], P('freq', None, None, 'tile')
Inputs may be any that keep to these rules, and one draw needn't show every extreme that they name: tile_ranks[f, i, j] is the rank of kernel tile (i, j) at frequency f. `row_order`: a permutation of the 64 kernel tile rows. `col_order`: a permutation of the 64 kernel tile columns.
All inputs are finite; a program needn't handle non-finite values.
Results may differ from a plain program's by a relative error of at most 0.0075.
Values may be sent and summed in bfloat16 or wider, within the bound.
A program may use at most 128 MiB of HBM per device.

v0:
```python
import jax
import jax.numpy as jnp
from jax import lax
from jax.experimental import pallas as pl
from jax.experimental.pallas import tpu as pltpu
from jax.sharding import PartitionSpec as P

MESH = pl.DeviceIdType.MESH
NX, NY, NC = 4, 4, 2
NT = NX * NY * NC
NF = 8
TILE = 256
RMAX = 48
SRC = 128
HS = SRC // 2
HL = 2 * HS
GD = NT // NX
GROWS = GD * 2 * RMAX


def kernel(
    sig_hbm, v_hbm, u_hbm, ranks_hbm, rows_hbm, cols_hbm, gate_hbm,
    fwd_out, adj_out,
    sig, v, u, w, b, send1, recv1, send2, recv2, acc, zs, zr, gs, gr,
    ranks, row_order, col_order, gate, sem_sig, sem_v, sem_u, sem_small,
    s1_send, s1_recv, s2_send, s2_recv, z1_send, z1_recv, z2_send, z2_recv,
):
    fr = lax.axis_index("freq")
    me = lax.axis_index("tile")
    core = lax.rem(me, NC)
    y = lax.rem(me // NC, NY)
    x = me // (NC * NY)

    sig_copy = pltpu.make_async_copy(sig_hbm.at[0], sig, sem_sig)
    sig_copy.start()
    small_copies = [
        pltpu.make_async_copy(ranks_hbm.at[0], ranks, sem_small.at[0]),
        pltpu.make_async_copy(rows_hbm, row_order, sem_small.at[1]),
        pltpu.make_async_copy(cols_hbm, col_order, sem_small.at[2]),
        pltpu.make_async_copy(gate_hbm, gate, sem_small.at[3]),
    ]
    for copy in small_copies:
        copy.start()

    def v_copy(g):
        rows = pl.ds(g * GD, GD)
        return pltpu.make_async_copy(v_hbm.at[0, rows], v.at[rows], sem_v.at[g])

    for i in range(NX):
        v_copy(lax.rem(x + 1 + i, NX)).start()

    barrier = pltpu.get_barrier_semaphore()
    for d in range(1, NT):
        pl.semaphore_signal(
            barrier, inc=1, device_id=(fr, lax.rem(me + d, NT)), device_id_type=MESH
        )
    for d in range(1, NF):
        pl.semaphore_signal(
            barrier, inc=1, device_id=(lax.rem(fr + d, NF), me), device_id_type=MESH
        )
    u_copy = pltpu.make_async_copy(u_hbm.at[0], u, sem_u)
    u_copy.start()

    sig_copy.wait()
    for l in range(2):
        cols = pl.ds(l * TILE, TILE)
        for h in range(2):
            src = pl.ds(h * HS, HS)
            re = sig[0, src, cols]
            im = sig[1, src, cols]
            w[l, pl.ds(h * HL, HS), pl.ds(0, TILE)] = re
            w[l, pl.ds(h * HL + HS, HS), pl.ds(0, TILE)] = im
            w[l, pl.ds(h * HL, HS), pl.ds(TILE, TILE)] = -im
            w[l, pl.ds(h * HL + HS, HS), pl.ds(TILE, TILE)] = re

    slots = lax.broadcasted_iota(jnp.int32, (RMAX, 1), 0)

    def factor_rows(factor, g, cols):
        return jnp.concatenate(
            [factor[pl.ds(g * GD, GD), :, p, :, cols].reshape(GROWS, TILE) for p in range(2)],
            axis=1,
        )

    def stage1(g):
        for l in range(2):
            col = col_order[me * 2 + l]
            out = lax.dot_general(
                factor_rows(v, g, pl.ds(l * TILE, TILE)),
                w[l],
                (((1,), (1,)), ((), ())),
                preferred_element_type=jnp.float32,
            )
            for i in range(2 * GD):
                rank = ranks[row_order[g * 2 * GD + i], col]
                part = out[i * RMAX : (i + 1) * RMAX]
                part = jnp.where(slots < rank, part, 0.0).astype(jnp.bfloat16)
                for h in range(2):
                    send1[2 * h + i % 2, g * GD + i // 2, l] = part[:, h * HL : (h + 1) * HL]

    def tile_copy(ex, c, other, slot):
        send, recv, sems, rsems = ex
        return pltpu.make_async_remote_copy(
            src_ref=send.at[c, other],
            dst_ref=recv.at[c, slot],
            send_sem=sems.at[c, other],
            recv_sem=rsems.at[c, slot],
            device_id=(fr, other),
            device_id_type=MESH,
        )

    ex1 = (send1, recv1, s1_send, s1_recv)
    ex2 = (send2, recv2, s2_send, s2_recv)

    def send_all(ex, c):
        def body(i, carry):
            dx = lax.rem(i, 4)
            px = lax.rem(x + dx, NX)
            py = lax.rem(y + dx + lax.rem(i // 4, 4), NY)
            tile_copy(ex, c, (px * NY + py) * NC + lax.rem(core + i // 16, NC), me).start()
            return carry

        lax.fori_loop(1, NT, body, 0)

    def wait_sends(ex, c):
        def body(d, carry):
            tile_copy(ex, c, lax.rem(me + d, NT), me).wait_send()
            return carry

        lax.fori_loop(1, NT, body, 0)

    def wait_from(ex, c, first, count):
        def body(i, carry):
            other = first + i

            @pl.when(other != me)
            def _():
                tile_copy(ex, c, other, other).wait_recv()

            return carry

        lax.fori_loop(0, count, body, 0)

    def first_group(i, carry):
        g = lax.rem(x + 1 + i, NX)
        v_copy(g).wait()
        stage1(g)

        @pl.when(i == 0)
        def _():
            pl.semaphore_wait(barrier, NT - 1 + NF - 1)

        def send_group(n, inner):
            other = g * GD + lax.rem(me + i + 1 + n, GD)

            @pl.when(other != me)
            def _():
                tile_copy(ex1, 0, other, me).start()

            return inner

        lax.fori_loop(0, GD, send_group, 0)
        return carry

    for copy in small_copies:
        copy.wait()
    lax.fori_loop(0, NX, first_group, 0)
    for c in range(1, 4):
        send_all(ex1, c)
    for c in range(4):
        recv1[c, me] = send1[c, me]

    def z_copy(src, dst, sems, rsems, c, other, slot):
        return pltpu.make_async_remote_copy(
            src_ref=src.at[c, other],
            dst_ref=dst.at[c, slot],
            send_sem=sems.at[c, other],
            recv_sem=rsems.at[c, slot],
            device_id=(other, me),
            device_id_type=MESH,
        )

    def z_start(src, dst, sems, rsems, c):
        def start(d, carry):
            z_copy(src, dst, sems, rsems, c, lax.rem(fr + d, NF), fr).start()
            return carry

        lax.fori_loop(1, NF, start, 0)
        dst[c, fr] = src[c, fr]

    def z_finish(src, dst, sems, rsems, c):
        def finish(d, carry):
            other = lax.rem(fr + d, NF)
            z_copy(src, dst, sems, rsems, c, other, other).wait()
            return carry

        lax.fori_loop(1, NF, finish, 0)

    def forward(c):
        cols = pl.ds((c % 2) * TILE, TILE)
        acc[0] = jnp.zeros_like(acc[0])

        def body(i, carry):
            g = lax.rem(x + i, NX)
            wait_from(ex1, c, g * GD, GD)
            acc[0] += lax.dot_general(
                recv1[c, pl.ds(g * GD, GD)].reshape(GROWS, HL),
                factor_rows(u, g, cols),
                (((0,), (0,)), ((), ())),
                preferred_element_type=jnp.float32,
            )
            return carry

        lax.fori_loop(0, NX, body, 0)

    def spread(c):
        h, k = c // 2, c % 2
        forward(c)
        rows, cols = pl.ds(h * HS, HS), pl.ds(k * TILE, TILE)
        re = (acc[0, 0:HS, 0:TILE] - acc[0, HS:HL, TILE:]).astype(jnp.bfloat16)
        im = (acc[0, HS:HL, 0:TILE] + acc[0, 0:HS, TILE:]).astype(jnp.bfloat16)
        fwd_out[0, 0, rows, cols] = re
        fwd_out[0, 1, rows, cols] = im
        for f in range(NF):
            m, n = (f // 2) * 16, (f % 2) * 128
            zs[c, f, 0] = re[m : m + 16, n : n + 128]
            zs[c, f, 1] = im[m : m + 16, n : n + 128]
        z_start(zs, zr, z1_send, z1_recv, c)

    def apply_gate(c):
        z_finish(zs, zr, z1_send, z1_recv, c)
        parts = [[zr[c, e, q].astype(jnp.float32) for q in range(2)] for e in range(NF)]
        for f in range(NF):
            re = jnp.zeros((16, 128), jnp.float32)
            im = jnp.zeros((16, 128), jnp.float32)
            for e in range(NF):
                p, q = gate[0, f, e], gate[1, f, e]
                re += p * parts[e][0] - q * parts[e][1]
                im += p * parts[e][1] + q * parts[e][0]
            gs[c, f, 0] = re.astype(jnp.bfloat16)
            gs[c, f, 1] = im.astype(jnp.bfloat16)
        z_start(gs, gr, z2_send, z2_recv, c)

    def project(c):
        k = c % 2
        cols = pl.ds(k * TILE, TILE)
        z_finish(gs, gr, z2_send, z2_recv, c)
        for e in range(NF):
            m, n = (e // 2) * 16, (e % 2) * 128
            re = gr[c, e, 0]
            im = gr[c, e, 1]
            b[m : m + 16, n : n + 128] = re
            b[HS + m : HS + m + 16, n : n + 128] = im
            b[m : m + 16, TILE + n : TILE + n + 128] = im
            b[HS + m : HS + m + 16, TILE + n : TILE + n + 128] = -re
        row = row_order[me * 2 + k]

        def stage3(g, carry):
            out = lax.dot_general(
                factor_rows(u, g, cols),
                b[...],
                (((1,), (1,)), ((), ())),
                preferred_element_type=jnp.float32,
            )
            for i in range(2 * GD):
                rank = ranks[row, col_order[g * 2 * GD + i]]
                part = out[i * RMAX : (i + 1) * RMAX]
                part = jnp.where(slots < rank, part, 0.0).astype(jnp.bfloat16)
                send2[c, g * GD + i // 2, i % 2] = part
            return carry

        lax.fori_loop(0, NX, stage3, 0)
        send_all(ex2, c)
        recv2[c, me] = send2[c, me]

    u_copy.wait()
    for c in range(4):
        spread(c)
        if c > 0:
            project(c - 1)
        apply_gate(c)
    project(3)

    for c in range(4):
        wait_sends(ex1, c)
    for c in range(4):
        h, k = c // 2, c % 2
        if k == 0:
            acc[...] = jnp.zeros_like(acc)
        if c == 3:
            for n in range(4):
                wait_sends(ex2, n)

        def adjoint(g, carry):
            devices = pl.ds(g * 2 * GD, 2 * GD)
            wait_from(ex2, c, g * 2 * GD, 2 * GD)
            for l in range(2):
                cols = pl.ds(l * TILE, TILE)
                rhs = jnp.concatenate(
                    [v[devices, k, p, :, cols].reshape(GROWS, TILE) for p in range(2)], axis=1
                )
                acc[l] += lax.dot_general(
                    recv2[c, devices, l].reshape(GROWS, HL),
                    rhs,
                    (((0,), (0,)), ((), ())),
                    preferred_element_type=jnp.float32,
                )
            return carry

        lax.fori_loop(0, 2, adjoint, 0)
        if k == 1:
            rows = pl.ds(h * HS, HS)
            for l in range(2):
                cols = pl.ds(l * TILE, TILE)
                re = acc[l, 0:HS, 0:TILE] + acc[l, HS:HL, TILE:]
                im = acc[l, HS:HL, 0:TILE] - acc[l, 0:HS, TILE:]
                adj_out[0, 0, rows, cols] = re.astype(jnp.bfloat16)
                adj_out[0, 1, rows, cols] = im.astype(jnp.bfloat16)


def shards(signal, v_factors, u_factors, tile_ranks, row_order, col_order, time_gate):
    bf16, f32 = jnp.bfloat16, jnp.float32
    block = (4, NT, 2, RMAX, HL)
    zblock = (4, NF, 2, 16, 128)
    factors = (NT, 2, 2, RMAX, 2 * TILE)
    hbm = pl.BlockSpec(memory_space=pltpu.HBM)
    dma = pltpu.SemaphoreType.DMA
    out = pltpu.VMEM((1, 2, SRC, 2 * TILE), bf16)
    vmem = pl.BlockSpec(memory_space=pltpu.VMEM)
    return pl.pallas_call(
        kernel,
        out_shape=(out, out),
        in_specs=[hbm] * 7,
        out_specs=(vmem, vmem),
        scratch_shapes=[
            pltpu.VMEM((2, SRC, 2 * TILE), bf16),
            pltpu.VMEM(factors, bf16),
            pltpu.VMEM(factors, bf16),
            pltpu.VMEM((2, 2 * SRC, 2 * TILE), bf16),
            pltpu.VMEM((HL, 2 * TILE), bf16),
            pltpu.VMEM(block, bf16),
            pltpu.VMEM(block, bf16),
            pltpu.VMEM(block, bf16),
            pltpu.VMEM(block, bf16),
            pltpu.VMEM((2, HL, 2 * TILE), f32),
            pltpu.VMEM(zblock, bf16),
            pltpu.VMEM(zblock, bf16),
            pltpu.VMEM(zblock, bf16),
            pltpu.VMEM(zblock, bf16),
            pltpu.SMEM(tile_ranks.shape[1:], jnp.int32),
            pltpu.SMEM(row_order.shape, jnp.int32),
            pltpu.SMEM(col_order.shape, jnp.int32),
            pltpu.SMEM(time_gate.shape, f32),
            dma,
            dma((NX,)),
            dma,
            dma((4,)),
            dma((4, NT)),
            dma((4, NT)),
            dma((4, NT)),
            dma((4, NT)),
            dma((4, NF)),
            dma((4, NF)),
            dma((4, NF)),
            dma((4, NF)),
        ],
        compiler_params=pltpu.CompilerParams(
            collective_id=0, has_side_effects=True, vmem_limit_bytes=66_500_000
        ),
        name="deconvolve",
    )(
        signal,
        v_factors.reshape((1,) + factors),
        u_factors.reshape((1,) + factors),
        tile_ranks,
        row_order,
        col_order,
        time_gate,
    )


def solution(mesh):
    return jax.shard_map(
        shards,
        mesh=mesh,
        in_specs=(
            P("freq", None, None, "tile"),
            P("freq", None, None, None, "tile"),
            P("freq", None, None, None, "tile"),
            P("freq", None, None),
            P(),
            P(),
            P(),
        ),
        out_specs=(P("freq", None, None, "tile"), P("freq", None, None, "tile")),
        check_vma=False,
    )
```

profile of v0, /device:TPU:1, one launch (start us, length us, event | category | flops | bytes accessed | tf_op | source)
XLA Modules:
  0.0 90.3 jit_solution(16634811148375591274)
XLA Ops:
  0.6 88.3 %deconvolve.1 = (bf16[1,2,128,512]{3,2,1,0:T(8,128)(2,1)S(1)}, bf16[1,2,128,512]{3,2,1,0:T(8,128)(2,1)S(1)}) custom-call(bf16[1,2,128,512]{3,2,1,0:T(8,128)(2,1)} %sig_hbm.1, bf16[1,32,2,2,48,512]{5,4,3,2,1,0:T(8,128)(2,1)} %bitcast.2, bf16[1,32,2,2,48,512]{5,4,3,2,1,0:T(8,128)(2,1)} %bitcast.3, s32[1,64,64]{2,1,0:T(8,128)} %ranks_hbm.1, s32[64]{0:T(128)} %rows_hbm.1, ...), custom_call_target="tpu_custom_call" | custom-call | tf_op jit(solution)/shard_map/deconvolve/pallas_call | solution.py:329
  88.9 0.7 copy.11
  89.6 0.7 copy.12
where the time goes:
time: 90.4 us; the launch traced here: 90.3 us
  Pallas kernels  88.3 us (98%)
  local copies, waits for them, and re-layouts  1.41 us (2%)
    pallas_call x1, Pallas kernels, shards(): pl.pallas_call(kernel, out_shape=(out, out), in_specs=[hbm] * 7, out_spec...  88.3 us

commit v1 on v0

--- a/solution.py
+++ b/solution.py
@@ -43,7 +43,7 @@
         copy.start()
 
     def v_copy(g):
-        rows = pl.ds(g * GD, GD)
+        rows = pl.ds(g * NY, NY)
         return pltpu.make_async_copy(v_hbm.at[0, rows], v.at[rows], sem_v.at[g])
 
     for i in range(NX):
@@ -77,7 +77,7 @@
 
     def factor_rows(factor, g, cols):
         return jnp.concatenate(
-            [factor[pl.ds(g * GD, GD), :, p, :, cols].reshape(GROWS, TILE) for p in range(2)],
+            [factor[pl.ds(g * NY, NY), :, :, p, :, cols].reshape(GROWS, TILE) for p in range(2)],
             axis=1,
         )
 
@@ -99,9 +99,10 @@
 
     def tile_copy(ex, c, other, slot):
         send, recv, sems, rsems = ex
+        place = recv.at[c, lax.rem(slot, NC), slot // NC]
         return pltpu.make_async_remote_copy(
             src_ref=send.at[c, other],
-            dst_ref=recv.at[c, slot],
+            dst_ref=place,
             send_sem=sems.at[c, other],
             recv_sem=rsems.at[c, slot],
             device_id=(fr, other),
@@ -128,9 +129,9 @@
 
         lax.fori_loop(1, NT, body, 0)
 
-    def wait_from(ex, c, first, count):
+    def wait_from_core(ex, c, par):
         def body(i, carry):
-            other = first + i
+            other = i * NC + par
 
             @pl.when(other != me)
             def _():
@@ -138,36 +139,23 @@
 
             return carry
 
-        lax.fori_loop(0, count, body, 0)
+        lax.fori_loop(0, NX * NY, body, 0)
 
     def first_group(i, carry):
         g = lax.rem(x + 1 + i, NX)
         v_copy(g).wait()
         stage1(g)
 
-        @pl.when(i == 0)
-        def _():
-            pl.semaphore_wait(barrier, NT - 1 + NF - 1)
-
-        def send_group(n, inner):
-            other = g * GD + lax.rem(me + i + 1 + n, GD)
-
-            @pl.when(other != me)
-            def _():
-                tile_copy(ex1, 0, other, me).start()
-
-            return inner
-
-        lax.fori_loop(0, GD, send_group, 0)
         return carry
 
     for copy in small_copies:
         copy.wait()
     lax.fori_loop(0, NX, first_group, 0)
-    for c in range(1, 4):
+    pl.semaphore_wait(barrier, NT - 1 + NF - 1)
+    for c in range(4):
         send_all(ex1, c)
     for c in range(4):
-        recv1[c, me] = send1[c, me]
+        recv1[c, core, me // NC] = send1[c, me]
 
     def z_copy(src, dst, sems, rsems, c, other, slot):
         return pltpu.make_async_remote_copy(
@@ -200,17 +188,20 @@
         acc[0] = jnp.zeros_like(acc[0])
 
         def body(i, carry):
-            g = lax.rem(x + i, NX)
-            wait_from(ex1, c, g * GD, GD)
+            par = lax.rem(core + i, NC)
+            wait_from_core(ex1, c, par)
+            rhs = jnp.concatenate(
+                [u[:, par, :, p, :, cols].reshape(2 * GROWS, TILE) for p in range(2)], axis=1
+            )
             acc[0] += lax.dot_general(
-                recv1[c, pl.ds(g * GD, GD)].reshape(GROWS, HL),
-                factor_rows(u, g, cols),
+                recv1[c, par].reshape(2 * GROWS, HL),
+                rhs,
                 (((0,), (0,)), ((), ())),
                 preferred_element_type=jnp.float32,
             )
             return carry
 
-        lax.fori_loop(0, NX, body, 0)
+        lax.fori_loop(0, NC, body, 0)
 
     def spread(c):
         h, k = c // 2, c % 2
@@ -270,7 +261,7 @@
 
         lax.fori_loop(0, NX, stage3, 0)
         send_all(ex2, c)
-        recv2[c, me] = send2[c, me]
+        recv2[c, core, me // NC] = send2[c, me]
 
     u_copy.wait()
     for c in range(4):
@@ -286,20 +277,19 @@
         h, k = c // 2, c % 2
         if k == 0:
             acc[...] = jnp.zeros_like(acc)
-        if c == 3:
-            for n in range(4):
-                wait_sends(ex2, n)
-
-        def adjoint(g, carry):
-            devices = pl.ds(g * 2 * GD, 2 * GD)
-            wait_from(ex2, c, g * 2 * GD, 2 * GD)
+        for n in ((), (), (0, 1), (2, 3))[c]:
+            wait_sends(ex2, n)
+
+        def adjoint(i, carry):
+            par = lax.rem(core + i, NC)
+            wait_from_core(ex2, c, par)
             for l in range(2):
                 cols = pl.ds(l * TILE, TILE)
                 rhs = jnp.concatenate(
-                    [v[devices, k, p, :, cols].reshape(GROWS, TILE) for p in range(2)], axis=1
+                    [v[:, par, k, p, :, cols].reshape(GROWS, TILE) for p in range(2)], axis=1
                 )
                 acc[l] += lax.dot_general(
-                    recv2[c, devices, l].reshape(GROWS, HL),
+                    recv2[c, par, :, l].reshape(GROWS, HL),
                     rhs,
                     (((0,), (0,)), ((), ())),
                     preferred_element_type=jnp.float32,
@@ -317,16 +307,28 @@
                 adj_out[0, 1, rows, cols] = im.astype(jnp.bfloat16)
 
 
+def write_out(fwd, adj, fwd_hbm, adj_hbm, sem):
+    copies = [
+        pltpu.make_async_copy(fwd, fwd_hbm, sem.at[0]),
+        pltpu.make_async_copy(adj, adj_hbm, sem.at[1]),
+    ]
+    for copy in copies:
+        copy.start()
+    for copy in copies:
+        copy.wait()
+
+
 def shards(signal, v_factors, u_factors, tile_ranks, row_order, col_order, time_gate):
     bf16, f32 = jnp.bfloat16, jnp.float32
     block = (4, NT, 2, RMAX, HL)
+    arrived = (4, NC, NX * NY, 2, RMAX, HL)
     zblock = (4, NF, 2, 16, 128)
-    factors = (NT, 2, 2, RMAX, 2 * TILE)
+    factors = (NX * NY, NC, 2, 2, RMAX, 2 * TILE)
     hbm = pl.BlockSpec(memory_space=pltpu.HBM)
     dma = pltpu.SemaphoreType.DMA
     out = pltpu.VMEM((1, 2, SRC, 2 * TILE), bf16)
     vmem = pl.BlockSpec(memory_space=pltpu.VMEM)
-    return pl.pallas_call(
+    fwd, adj = pl.pallas_call(
         kernel,
         out_shape=(out, out),
         in_specs=[hbm] * 7,
@@ -338,9 +340,9 @@
             pltpu.VMEM((2, 2 * SRC, 2 * TILE), bf16),
             pltpu.VMEM((HL, 2 * TILE), bf16),
             pltpu.VMEM(block, bf16),
+            pltpu.VMEM(arrived, bf16),
             pltpu.VMEM(block, bf16),
-            pltpu.VMEM(block, bf16),
-            pltpu.VMEM(block, bf16),
+            pltpu.VMEM(arrived, bf16),
             pltpu.VMEM((2, HL, 2 * TILE), f32),
             pltpu.VMEM(zblock, bf16),
             pltpu.VMEM(zblock, bf16),
@@ -376,6 +378,16 @@
         col_order,
         time_gate,
     )
+    out = jax.ShapeDtypeStruct((1, 2, SRC, 2 * TILE), bf16)
+    return pl.pallas_call(
+        write_out,
+        out_shape=(out, out),
+        in_specs=[vmem, vmem],
+        out_specs=(pl.BlockSpec(memory_space=pltpu.HBM),) * 2,
+        scratch_shapes=[dma((2,))],
+        compiler_params=pltpu.CompilerParams(vmem_limit_bytes=2**20),
+        name="write_out",
+    )(fwd, adj)
 
 
 def solution(mesh):

time: 90.4 us -> 89.6 us (level)
  local copies, waits for them, and re-layouts: 1.41 us -> 0 us
    unnamed x2 -> x0, local copies, waits for them, and re-layouts: 1.41 us -> none
where the time goes in v1:
time: 89.6 us; the launch traced here: 89.5 us
  Pallas kernels  88.8 us (99%)
    pallas_call x1, Pallas kernels, shards(): pl.pallas_call(kernel, out_shape=(out, out), in_specs=[hbm] * 7, out_spec...  88 us

profile of v1, /device:TPU:1, one launch (start us, length us, event | category | flops | bytes accessed | tf_op | source)
XLA Modules:
  0.0 89.5 jit_solution(15776440304624072439)
XLA Ops:
  0.6 88.0 %deconvolve.1 = (bf16[1,2,128,512]{3,2,1,0:T(8,128)(2,1)S(1)}, bf16[1,2,128,512]{3,2,1,0:T(8,128)(2,1)S(1)}) custom-call(bf16[1,2,128,512]{3,2,1,0:T(8,128)(2,1)} %sig_hbm.1, bf16[1,16,2,2,2,48,512]{6,5,4,3,2,1,0:T(8,128)(2,1)} %bitcast.2, bf16[1,16,2,2,2,48,512]{6,5,4,3,2,1,0:T(8,128)(2,1)} %bitcast.3, s32[1,64,64]{2,1,0:T(8,128)} %ranks_hbm.1, ...), custom_call_target="tpu_custom_call" | custom-call | tf_op jit(solution)/shard_map/deconvolve/pallas_call | solution.py:331
  88.7 0.8 write_out.1

commit v2 on v1

--- a/solution.py
+++ b/solution.py
@@ -16,6 +16,15 @@
 HL = 2 * HS
 GD = NT // NX
 GROWS = GD * 2 * RMAX
+
+MIXED = [
+    (dx, (step + dx % 2) % NY, dc)
+    for dc in range(NC)
+    for step in (2, 1, 3, 0)
+    for dx in (1, 3, 2, 0)
+    if (dx, (step + dx % 2) % NY, dc) != (0, 0, 0)
+]
+FAR = sorted(MIXED, key=lambda v: (v[2], -min(v[0], NX - v[0]) - min(v[1], NY - v[1])))
 
 
 def kernel(
@@ -112,15 +121,10 @@
     ex1 = (send1, recv1, s1_send, s1_recv)
     ex2 = (send2, recv2, s2_send, s2_recv)
 
-    def send_all(ex, c):
-        def body(i, carry):
-            dx = lax.rem(i, 4)
-            px = lax.rem(x + dx, NX)
-            py = lax.rem(y + dx + lax.rem(i // 4, 4), NY)
-            tile_copy(ex, c, (px * NY + py) * NC + lax.rem(core + i // 16, NC), me).start()
-            return carry
-
-        lax.fori_loop(1, NT, body, 0)
+    def send_all(ex, c, order=MIXED):
+        for dx, dy, dc in order:
+            chip = lax.rem(x + dx, NX) * NY + lax.rem(y + dy, NY)
+            tile_copy(ex, c, chip * NC + lax.rem(core + dc, NC), me).start()
 
     def wait_sends(ex, c):
         def body(d, carry):
@@ -260,7 +264,7 @@
             return carry
 
         lax.fori_loop(0, NX, stage3, 0)
-        send_all(ex2, c)
+        send_all(ex2, c, FAR if c == 3 else MIXED)
         recv2[c, core, me // NC] = send2[c, me]
 
     u_copy.wait()

time: 89.6 us -> 88.8 us (level)
  no operation moved by 1% of the time
where the time goes in v2:
time: 88.8 us; the launch traced here: 88.7 us
  Pallas kernels  88.1 us (99%)
    pallas_call x1, Pallas kernels, shards(): pl.pallas_call(kernel, out_shape=(out, out), in_specs=[hbm] * 7, out_spec...  87.2 us

profile of v2, /device:TPU:1, one launch (start us, length us, event | category | flops | bytes accessed | tf_op | source)
XLA Modules:
  0.0 88.7 jit_solution(16224791436126867712)
XLA Ops:
  0.6 87.2 %deconvolve.1 = (bf16[1,2,128,512]{3,2,1,0:T(8,128)(2,1)S(1)}, bf16[1,2,128,512]{3,2,1,0:T(8,128)(2,1)S(1)}) custom-call(bf16[1,2,128,512]{3,2,1,0:T(8,128)(2,1)} %sig_hbm.1, bf16[1,16,2,2,2,48,512]{6,5,4,3,2,1,0:T(8,128)(2,1)} %bitcast.2, bf16[1,16,2,2,2,48,512]{6,5,4,3,2,1,0:T(8,128)(2,1)} %bitcast.3, s32[1,64,64]{2,1,0:T(8,128)} %ranks_hbm.1, ...), custom_call_target="tpu_custom_call" | custom-call | tf_op jit(solution)/shard_map/deconvolve/pallas_call | solution.py:335
  87.9 0.8 write_out.1
